TPU v7x, 32 devices: a whole 2x2x4 slice. The times are simulated.
32 devices in a mesh: pair: 2 (over core), row: 16 (over z, y, x).
Axes of the slice: x: 2, y: 2, z: 4, core: 2. Of those that a mesh axis runs over, the one named last changes fastest.
Arguments:
- snapshot: float32 [4096, 1024], P('row', 'pair'), may hold values from -6 to 6
- weights: float32 [8, 128], replicated, may hold values from 0 to 1
- block_home: int32 [8], P('pair'), may hold values from 0 to 7, each once
- plan: int32 [2, 2, 4], P(None, 'pair'), may hold values from 0 to 3, each once within a row
Outputs:
- rotated: float32 [4096, 1024], P('row', 'pair')
- column_norms: float32 [1024], P('pair')
All inputs are finite; a program needn't handle non-finite values. Where the computation divides by a largest or mean magnitude, that divisor is 1e-20 or more.
Results may differ from a plain program's by a relative error of at most 0.0001.
Values sent between devices are 32-bit elements; how exact they have to be, the bound alone decides.
No kernel may reach another device: no remote copies, remote signals or barrier semaphores. Data moves between devices by JAX's collectives and lax.ppermute only.
A program may use at most 128 MiB of HBM per device.

v0:
```python
import jax
import jax.numpy as jnp
from jax import lax
from jax.sharding import PartitionSpec as P

epsilon = 1e-06
step_size = 4.0
newton_turns = 5
highest = lax.Precision.HIGHEST


def shifted(block, axis, distance):
    devices = range(lax.axis_size(axis))
    route = [((i - distance) % len(devices), i) for i in devices]
    return lax.ppermute(block, axis, route)


def rotation(gram_matrix, spread):
    diagonal_part = jnp.diagonal(gram_matrix, axis1=1, axis2=2)
    inverse = lax.rsqrt(diagonal_part + epsilon)
    corr = gram_matrix * inverse[:, :, None] * inverse[:, None, :]
    skew_part = step_size * corr * (spread[:, :, None] - spread[:, None, :])
    row_bound = 1.0 + jnp.max(jnp.sum(jnp.abs(skew_part), axis=2), axis=1)
    unit_matrix = jnp.eye(gram_matrix.shape[1], dtype=jnp.float32)
    current = unit_matrix[None] + skew_part / row_bound[:, None, None]
    for index in range(newton_turns):
        inner_gram = jnp.einsum("pcd,pce->pde", current, current, precision=highest)
        current = jnp.einsum(
            "pcd,pde->pce", current, 1.5 * unit_matrix[None] - 0.5 * inner_gram, precision=highest
        )
    return current


def full_gram(paired):
    local_gram = jnp.einsum("rpc,rpd->pcd", paired, paired, precision=highest)
    return lax.psum(local_gram, "row")


def assemble(carried, cross_gram):
    first_diag = carried[0::2]
    second = carried[1::2]
    upper_rows = jnp.concatenate([first_diag, cross_gram], axis=2)
    lower_rows = jnp.concatenate([jnp.swapaxes(cross_gram, 1, 2), second], axis=2)
    return jnp.concatenate([upper_rows, lower_rows], axis=1)


def body(snapshot, weights, block_home, plan):
    row_count = snapshot.shape[0]
    block_width = weights.shape[1]
    slot_count = block_home.shape[0]
    rounds = plan.shape[0]
    blocks_here = snapshot.reshape(row_count, slot_count, block_width)
    spread = jnp.take(weights, block_home, axis=0)
    carried = jnp.zeros((slot_count, block_width, block_width), jnp.float32)
    for round_index in range(rounds):
        ordering = plan[round_index, 0]
        blocks_here = jnp.take(blocks_here, ordering, axis=1)
        spread = jnp.take(spread, ordering, axis=0)
        paired = blocks_here.reshape(row_count, 2, 2 * block_width)
        if round_index == 0:
            gram_matrix = full_gram(paired)
        else:
            carried = jnp.take(carried, ordering, axis=0)
            local_cross = jnp.einsum(
                "rpc,rpd->pcd", blocks_here[:, 0::2], blocks_here[:, 1::2], precision=highest
            )
            cross_gram = lax.psum(local_cross, "row")
            gram_matrix = assemble(carried, cross_gram)
        turn_matrix = rotation(gram_matrix, spread.reshape(2, 2 * block_width))
        result = jnp.einsum("rpc,pcd->rpd", paired, turn_matrix, precision=highest)
        blocks_here = result.reshape(row_count, slot_count, block_width)
        gram_times = jnp.einsum("pcd,pde->pce", gram_matrix, turn_matrix, precision=highest)
        rotated_gram = jnp.einsum("pcd,pce->pde", turn_matrix, gram_times, precision=highest)
        carried = jnp.stack(
            [
                rotated_gram[:, :block_width, :block_width],
                rotated_gram[:, block_width:, block_width:],
            ],
            axis=1,
        ).reshape(slot_count, block_width, block_width)
        ahead_block, ahead_scale, ahead_own = shifted(
            (blocks_here[:, 0], spread[0], carried[0]), "pair", 1
        )
        behind_block, behind_scale, behind_own = shifted(
            (blocks_here[:, 3], spread[3], carried[3]), "pair", -1
        )
        carried = jnp.stack([ahead_own, carried[1], carried[2], behind_own], axis=0)
        blocks_here = jnp.stack(
            [ahead_block, blocks_here[:, 1], blocks_here[:, 2], behind_block], axis=1
        )
        spread = jnp.stack([ahead_scale, spread[1], spread[2], behind_scale], axis=0)
    final_matrix = blocks_here.reshape(row_count, slot_count * block_width)
    squares = jnp.diagonal(carried, axis1=1, axis2=2).reshape(slot_count * block_width)
    return (final_matrix, jnp.sqrt(squares))


def solution(mesh):
    in_specs = (P("row", "pair"), P(), P("pair"), P(None, "pair", None))
    out_specs = (P("row", "pair"), P("pair"))
    return jax.shard_map(body, mesh=mesh, in_specs=in_specs, out_specs=out_specs, check_vma=False)
```

profile of v0, /device:TPU:0, one launch (start us, length us, event | category | flops | bytes accessed | tf_op | source)
XLA Modules:
  0.0 318.9 jit_solution(17270181886986516772)
XLA Ops:
  11.1 1.2 copy.124
  13.5 1.5 fusion.21
  16.5 110.4 %all-reduce.3.cloned.1.call-done = f32[2,256,256]{2,1,0:T(8,128)} async-done(((f32[2,256,256]{2,1,0:T(8,128)}), f32[2,256,256]{2,1,0:T(8,128)}) %all-reduce.3.cloned.1.call-update) | async-done | bytes 524304 | tf_op jit(solution)/shard_map/psum | solution.py:36
  126.9 17.3 %copy.128 = f32[2,256,256]{0,2,1:T(8,128)} copy(f32[2,256,256]{2,1,0:T(8,128)} %all-reduce.3.cloned.1.call-done) | data formatting | bytes 1048576 | tf_op jit(solution)/shard_map/psum | solution.py:36
  144.2 2.3 gather_fusion
  147.1 1.4 fusion.9
  149.3 1.1 fusion.8
  151.1 1.1 fusion.7
  152.8 1.1 fusion.6
  154.6 1.1 fusion.5
  158.1 1.3 fusion.27
  162.8 1.3 fusion.10
  164.4 104.3 %all-reduce.5.cloned.1.call-done = f32[2,128,128]{2,1,0:T(8,128)} async-done(((f32[2,128,128]{2,1,0:T(8,128)}), f32[2,128,128]{2,1,0:T(8,128)}) %all-reduce.5.cloned.1.call-update) | async-done | bytes 131088 | tf_op jit(solution)/shard_map/psum | solution.py:67
  270.7 16.6 %copy.145 = f32[2,256,256]{0,2,1:T(8,128)} copy(f32[2,256,256]{2,1,0:T(8,128)S(1)} %maximum_maximum_fusion) | data formatting | bytes 1048576 | tf_op jit(solution)/shard_map/concatenate | solution.py:44
  287.3 2.3 gather_fusion.3
  290.2 1.4 fusion.4
  292.4 1.1 fusion.3
  294.2 1.1 fusion.2
  295.9 1.1 fusion.1
  297.7 1.1 fusion
  299.5 1.1 fusion.33
  301.2 1.1 fusion.34
  303.9 4.6 %copy.159 = f32[4,128,128]{0,2,1:T(8,128)} copy(f32[4,128,128]{2,1,0:T(8,128)S(1)} %pad_maximum_fusion.5) | data formatting | bytes 524288 | tf_op jit(solution)/shard_map/stack | solution.py:87
  308.5 1.8 gather_fusion.4
  (114 shorter events, 25.7 us)
Async XLA Ops:
  7.2 2.1 copy-start
  7.2 119.7 %all-reduce.3.cloned.1.call-start = ((), (), s32[]{:S(2)}) async-start(), calls=%async_computation | async-start | bytes 1048576 | tf_op jit(solution)/shard_map/psum | solution.py:36
  10.5 5.2 %collective-permute-start.5 = (f32[128]{0:T(128)S(1)}, f32[128]{0:T(128)S(1)}, u32[]{:S(2)}, u32[]{:S(2)}) collective-permute-start(f32[128]{0:T(128)S(1)} %get-tuple-element.23), channel_id=1, source_target_pairs={{16,0},{0,16},{17,1},{1,17},{18,2},{2,18},{19,3},{3,19},{20,4},{4,... | collective-permute-start | bytes 1544 | tf_op jit(solution)/shard_map/ppermute | solution.py:15
  11.0 4.8 %collective-permute-start.4 = (f32[128]{0:T(128)S(1)}, f32[128]{0:T(128)S(1)}, u32[]{:S(2)}, u32[]{:S(2)}) collective-permute-start(f32[128]{0:T(128)S(1)} %get-tuple-element.22), channel_id=1, source_target_pairs={{16,0},{0,16},{17,1},{1,17},{18,2},{2,18},{19,3},{3,19},{20,4},{4,... | collective-permute-start | bytes 1544 | tf_op jit(solution)/shard_map/ppermute | solution.py:15
  14.9 253.7 %all-reduce.5.cloned.1.call-start = ((), (), s32[]{:S(2)}) async-start(), calls=%async_computation.1 | async-start | bytes 262144 | tf_op jit(solution)/shard_map/psum | solution.py:67
  126.9 19.8 %copy-start.2 = (f32[2,256,256]{2,1,0:T(8,128)S(1)}, f32[2,256,256]{2,1,0:T(8,128)}, u32[]{:S(2)}) copy-start(f32[2,256,256]{2,1,0:T(8,128)} %all-reduce.3.cloned.1.call-done) | copy-start | bytes 1572868
  159.5 1.6 collective-permute-start.1
  159.6 1.5 collective-permute-start
  160.2 1.6 collective-permute-start.3
  160.6 1.5 collective-permute-start.2
  268.7 21.0 %copy-start.3 = (f32[2,128,128]{2,1,0:T(8,128)S(1)}, f32[2,128,128]{2,1,0:T(8,128)}, u32[]{:S(2)}) copy-start(f32[2,128,128]{2,1,0:T(8,128)} %all-reduce.5.cloned.1.call-done) | copy-start | bytes 393220
  269.8 42.3 %copy-start.1 = (f32[8,128]{1,0:T(8,128)S(1)}, f32[8,128]{1,0:T(8,128)}, u32[]{:S(2)}) copy-start(f32[8,128]{1,0:T(8,128)} %param.9) | copy-start | bytes 12292
  302.4 1.3 collective-permute-start.9
  302.5 1.4 collective-permute-start.8
  303.0 8.0 %collective-permute-start.7 = (f32[256,128]{0,1:T(8,128)S(1)}, f32[256,128]{0,1:T(8,128)S(1)}, u32[]{:S(2)}, u32[]{:S(2)}) collective-permute-start(f32[256,128]{0,1:T(8,128)S(1)} %get-tuple-element.11), channel_id=1, source_target_pairs={{16,0},{0,16},{17,1},{1,17},{18,2},{2,18},{19,3},{3,19},{20,4},{4,... | collective-permute-start | bytes 393224 | tf_op jit(solution)/shard_map/ppermute | solution.py:15
  303.2 7.8 %collective-permute-start.6 = (f32[256,128]{0,1:T(8,128)S(1)}, f32[256,128]{0,1:T(8,128)S(1)}, u32[]{:S(2)}, u32[]{:S(2)}) collective-permute-start(f32[256,128]{0,1:T(8,128)S(1)} %get-tuple-element.10), channel_id=1, source_target_pairs={{16,0},{0,16},{17,1},{1,17},{18,2},{2,18},{19,3},{3,19},{20,4},{4,... | collective-permute-start | bytes 393224 | tf_op jit(solution)/shard_map/ppermute | solution.py:15
Sparse Core Ops, SparseCore 0:
  15.1 111.7 all-reduce.2
  164.3 104.3 all-reduce.4
where the time goes:
time: 320 us; the launch traced here: 319 us
  waiting for transfers between devices  215 us (67%)
  local copies, waits for them, and re-layouts  53.7 us (17%)
  matrix products  26.9 us (8%)
  between operations  14.6 us (5%)
  other arithmetic  5.34 us (2%)
    psum x1, waiting for transfers between devices, full_gram(): return lax.psum(local_gram, 'row')  110 us
    psum x1, waiting for transfers between devices, body(): cross_gram = lax.psum(local_cross, 'row')  104 us
    psum x1, local copies, waits for them, and re-layouts, full_gram(): return lax.psum(local_gram, 'row')  17.3 us
    concatenate x1, local copies, waits for them, and re-layouts, assemble(): return jnp.concatenate([upper_rows, lower_rows], axis=1)  16.6 us
    dot_general x10, matrix products, rotation(): inner_gram = jnp.einsum('pcd,pce->pde', current, current, precision=highest)  11.4 us
    dot_general x10, matrix products, rotation(): jnp.einsum('pcd,pde->pce', current, 1.5 * unit_matrix[None] - 0.5 * inner...  6.9 us
  transfers between devices with their start and end apart: 12, of which 5 were waited for; matrix products, arithmetic and copies ran while one was open for 4% of the time, Pallas kernels for 0%

commit v1 on v0

--- a/solution.py
+++ b/solution.py
@@ -7,6 +7,12 @@
 step_size = 4.0
 newton_turns = 5
 highest = lax.Precision.HIGHEST
+
+
+def summed_here(x, axis):
+    pieces = lax.all_gather(x, axis, axis=0, tiled=False)
+    total = pieces.sum(axis=0)
+    return total
 
 
 def shifted(block, axis, distance):
@@ -64,7 +70,7 @@
             local_cross = jnp.einsum(
                 "rpc,rpd->pcd", blocks_here[:, 0::2], blocks_here[:, 1::2], precision=highest
             )
-            cross_gram = lax.psum(local_cross, "row")
+            cross_gram = summed_here(local_cross, "row")
             gram_matrix = assemble(carried, cross_gram)
         turn_matrix = rotation(gram_matrix, spread.reshape(2, 2 * block_width))
         result = jnp.einsum("rpc,pcd->rpd", paired, turn_matrix, precision=highest)

time: 320 us -> 270 us (0.84)
  waiting for transfers between devices: 215 us -> 167 us
    psum x1 -> x0, waiting for transfers between devices: 104 us -> none  [body(): cross_gram = lax.psum(local_cross, 'row')]
    all_gather x0 -> x1, waiting for transfers between devices: none -> 53 us  [summed_here(): pieces = lax.all_gather(x, axis, axis=0, tiled=False)]
  transfers between devices with their start and end apart: 12 -> 12, of which waited for: 5 -> 10; matrix products, arithmetic and copies ran while one was open for 4% -> 5% of each run, Pallas kernels for 0% -> 0%
where the time goes in v1:
time: 270 us
  waiting for transfers between devices  167 us (62%)
  local copies, waits for them, and re-layouts  52.7 us (20%)
  matrix products  26.7 us (10%)
  between operations  14.6 us (5%)
  other arithmetic  5.48 us (2%)
  starting transfers between devices  3.12 us (1%)
    psum x1, waiting for transfers between devices, full_gram(): return lax.psum(local_gram, 'row')  111 us
    all_gather x1, waiting for transfers between devices, summed_here(): pieces = lax.all_gather(x, axis, axis=0, tiled=False)  53 us
    psum x1, local copies, waits for them, and re-layouts, full_gram(): return lax.psum(local_gram, 'row')  17.3 us
    concatenate x1, local copies, waits for them, and re-layouts, assemble(): return jnp.concatenate([upper_rows, lower_rows], axis=1)  16.6 us
    dot_general x10, matrix products, rotation(): inner_gram = jnp.einsum('pcd,pce->pde', current, current, precision=highest)  11.5 us
    dot_general x10, matrix products, rotation(): jnp.einsum('pcd,pde->pce', current, 1.5 * unit_matrix[None] - 0.5 * inner...  6.9 us
  transfers between devices with their start and end apart: 12, of which 10 were waited for; matrix products, arithmetic and copies ran while one was open for 5% of the time, Pallas kernels for 0%

profile of v1, /device:TPU:0, one launch (start us, length us, event | category | flops | bytes accessed | tf_op | source)
XLA Modules:
  0.0 269.6 jit_solution(9353111588366096347)
XLA Ops:
  7.9 1.2 copy.124
  10.3 1.5 fusion.21
  14.5 111.1 %all-reduce.2.cloned.1.call-done = f32[2,256,256]{2,1,0:T(8,128)} async-done(((f32[2,256,256]{2,1,0:T(8,128)}), f32[2,256,256]{2,1,0:T(8,128)}) %all-reduce.2.cloned.1.call-update) | async-done | bytes 524304 | tf_op jit(solution)/shard_map/psum | solution.py:42
  125.6 17.3 %copy.128 = f32[2,256,256]{0,2,1:T(8,128)} copy(f32[2,256,256]{2,1,0:T(8,128)} %all-reduce.2.cloned.1.call-done) | data formatting | bytes 1048576 | tf_op jit(solution)/shard_map/psum | solution.py:42
  142.9 2.3 gather_fusion
  145.8 1.4 fusion.9
  148.0 1.1 fusion.8
  149.8 1.1 fusion.7
  151.6 1.1 fusion.6
  153.3 1.1 fusion.5
  158.7 1.3 fusion.10
  166.6 53.0 %all-gather.3.cloned.1.call-done = f32[32,128,128]{2,1,0:T(8,128)} async-done(((f32[2,128,128]{2,1,0:T(8,128)}), f32[32,128,128]{2,1,0:T(8,128)}) %all-gather.3.cloned.1.call-update) | async-done | bytes 2097168 | tf_op jit(solution)/shard_map/all_gather | solution.py:13
  219.6 1.7 reduce_sum.28
  221.5 16.6 %copy.145 = f32[2,256,256]{0,2,1:T(8,128)} copy(f32[2,256,256]{2,1,0:T(8,128)S(1)} %maximum_maximum_fusion) | data formatting | bytes 1048576 | tf_op jit(solution)/shard_map/concatenate | solution.py:50
  238.0 2.3 gather_fusion.3
  240.9 1.4 fusion.4
  243.2 1.1 fusion.3
  244.9 1.1 fusion.2
  246.7 1.1 fusion.1
  248.4 1.1 fusion
  250.9 1.1 fusion.33
  251.9 1.1 fusion.34
  254.6 4.6 %copy.159 = f32[4,128,128]{0,2,1:T(8,128)} copy(f32[4,128,128]{2,1,0:T(8,128)S(1)} %pad_maximum_fusion.5) | data formatting | bytes 524288 | tf_op jit(solution)/shard_map/stack | solution.py:93
  259.3 1.8 gather_fusion.4
  (115 shorter events, 26.6 us)
Async XLA Ops:
  7.2 6.0 %copy-start = (f32[8,128]{1,0:T(8,128)S(1)}, f32[8,128]{1,0:T(8,128)}, u32[]{:S(2)}) copy-start(f32[8,128]{1,0:T(8,128)} %param.9) | copy-start | bytes 12292
  7.2 118.4 %all-reduce.2.cloned.1.call-start = ((), (), s32[]{:S(2)}) async-start(), calls=%async_computation | async-start | bytes 1048576 | tf_op jit(solution)/shard_map/psum | solution.py:42
  10.0 150.8 %copy-start.3 = (s32[2,1,4]{2,1,0:T(1,128)S(1)}, s32[2,1,4]{2,1,0:T(1,128)}, u32[]{:S(2)}) copy-start(s32[2,1,4]{2,1,0:T(1,128)} %param.11) | copy-start | bytes 100
  11.8 207.8 %all-gather.3.cloned.1.call-start = ((), (), s32[]{:S(2)}) async-start(), calls=%async_computation.1 | async-start | bytes 2228224 | tf_op jit(solution)/shard_map/all_gather | solution.py:13
  125.6 19.8 %copy-start.2 = (f32[2,256,256]{2,1,0:T(8,128)S(1)}, f32[2,256,256]{2,1,0:T(8,128)}, u32[]{:S(2)}) copy-start(f32[2,256,256]{2,1,0:T(8,128)} %all-reduce.2.cloned.1.call-done) | copy-start | bytes 1572868
  156.3 1.4 collective-permute-start.3
  156.4 1.5 collective-permute-start.2
  160.1 1.3 collective-permute-start.5
  160.5 1.2 collective-permute-start.4
  164.1 1.3 collective-permute-start.1
  164.4 1.3 collective-permute-start
  221.4 41.4 %copy-start.1 = (f32[8,128]{1,0:T(8,128)S(1)}, f32[8,128]{1,0:T(8,128)}, u32[]{:S(2)}) copy-start(f32[8,128]{1,0:T(8,128)} %param.9) | copy-start | bytes 12292
  253.1 1.3 collective-permute-start.9
  253.2 1.4 collective-permute-start.8
  253.8 8.0 %collective-permute-start.7 = (f32[256,128]{0,1:T(8,128)S(1)}, f32[256,128]{0,1:T(8,128)S(1)}, u32[]{:S(2)}, u32[]{:S(2)}) collective-permute-start(f32[256,128]{0,1:T(8,128)S(1)} %get-tuple-element.11), channel_id=1, source_target_pairs={{16,0},{0,16},{17,1},{1,17},{18,2},{2,18},{19,3},{3,19},{20,4},{4,... | collective-permute-start | bytes 393224 | tf_op jit(solution)/shard_map/ppermute | solution.py:21
  253.9 7.8 %collective-permute-start.6 = (f32[256,128]{0,1:T(8,128)S(1)}, f32[256,128]{0,1:T(8,128)S(1)}, u32[]{:S(2)}, u32[]{:S(2)}) collective-permute-start(f32[256,128]{0,1:T(8,128)S(1)} %get-tuple-element.10), channel_id=1, source_target_pairs={{16,0},{0,16},{17,1},{1,17},{18,2},{2,18},{19,3},{3,19},{20,4},{4,... | collective-permute-start | bytes 393224 | tf_op jit(solution)/shard_map/ppermute | solution.py:21
Sparse Core Ops, SparseCore 0:
  13.7 111.8 all-reduce.1
  160.2 59.3 all-gather.2
